TPU v7x, 256 devices: a whole 4x4x8 slice. The times are simulated.
256 devices in a mesh: feat: 64 (over z, y, x_hi), row: 2 (over x_lo), col: 2 (over core).
Axes of the slice: x: 4 (x_hi: 2, x_lo: 2; x = x_hi * 2 + x_lo), y: 4, z: 8, core: 2. Of those that a mesh axis runs over, the one named last changes fastest.
Arguments:
- local_x: float32 [4, 256, 256], P(('row', 'col'), 'feat'), may hold values from -4 to 4
- dual_var: float32 [4, 256, 256], P(('row', 'col'), 'feat'), may hold values from -2 to 2
- consensus_old: float32 [256, 256], P('feat'), may hold values from -4 to 4
- blocks_data: bfloat16 [4, 256, 512, 256], P(('row', 'col'), 'feat'), may hold values from -0.375 to 0.375
- row_index: int32 [4, 256, 512], P(('row', 'col'), 'feat'), may hold values from 0 to 16383, as said below
- labels: int32 [4, 16384], P(('row', 'col')), may hold values 0 or 1
Outputs:
- solved_x: float32 [4, 256, 256], P(('row', 'col'), 'feat')
- dual_new: float32 [4, 256, 256], P(('row', 'col'), 'feat')
- consensus: float32 [256, 256], P('feat')
- norms: float32 [2], replicated
Inputs may be any that keep to these rules, and one draw needn't show every extreme that they name: `row_index`: the 512 rows of one block are distinct samples of its shard; a sample may appear in no block or in several.
All inputs are finite; a program needn't handle non-finite values. No bound on the sum of `labels` on one device may be relied on, other than what follows from the above.
Results may differ from a plain program's by a relative error of at most 0.0019.
Values sent between devices are 32-bit elements; how exact they have to be, the bound alone decides.
No kernel may reach another device: no remote copies, remote signals or barrier semaphores. Data moves between devices by JAX's collectives and lax.ppermute only.
A program may use at most 64 MiB of HBM per device.

v0:
```python
import jax
import jax.numpy as jnp
from jax import lax
from jax.sharding import Mesh
from jax.sharding import PartitionSpec as P

NEWTON_STEPS = 2
CG_STEPS = 3
FEAT = ("feat_0", "feat_1", "feat_2")
FEAT_ROW_COL = ("feat_0", "feat_1", "feat_2", "row", "col")
penalty = 1.0
damping = 0.5
threshold = 0.05


def filled_up(lines, size):
    spare = -len(lines) % size
    return jnp.pad(lines, [(0, spare)] + [(0, 0)] * (lines.ndim - 1))


def copy_for_each(x, axis):
    copies = jnp.broadcast_to(x, (lax.axis_size(axis), *x.shape))
    return lax.all_to_all(copies, axis, split_axis=0, concat_axis=0, tiled=True)


def joined_along(parts, dim):
    parts = jnp.moveaxis(parts, 0, dim)
    dims = parts.shape
    return parts.reshape(*dims[:dim], dims[dim] * dims[dim + 1], *dims[dim + 2 :])


def gather_directly(x, axis, dim):
    parts = copy_for_each(x, axis)
    return joined_along(parts, dim)


def cut_along(x, dim, size):
    before, after = (x.shape[:dim], x.shape[dim + 1 :])
    return jnp.moveaxis(x.reshape(*before, size, -1, *after), dim, 0)


def summed_on_arrival(x, axis, dim):
    size = lax.axis_size(axis)
    parts = lax.all_to_all(cut_along(x, dim, size), axis, 0, 0, tiled=True)
    return jnp.sum(parts, axis=0)


def total_of(x, axes):
    lines = x.reshape(-1)
    padded = filled_up(lines, lax.axis_size(axes))
    whole = gather_directly(summed_on_arrival(padded, axes, 0), axes, 0)
    return lax.slice_in_dim(whole, 0, len(lines)).reshape(x.shape)


def of_everyone(x, axis):
    everything = copy_for_each(x, axis)
    return jnp.sum(everything, axis=0)


def by_axis(x, axes):
    for axis in axes:
        x = lax.psum(x, axis)
    return x


def shrink(values):
    return jnp.sign(values) * jnp.maximum(jnp.abs(values) - threshold, 0.0)


def conjugate_solve(hessian, gradient):
    delta = jnp.zeros_like(gradient)
    residual = gradient
    direction = gradient
    power = jnp.sum(residual * residual, axis=1)
    for cg_step in range(CG_STEPS):
        image = jnp.einsum("bkl,bl->bk", hessian, direction, precision=lax.Precision.HIGHEST)
        alpha = power / jnp.sum(direction * image, axis=1)
        delta = delta + alpha[:, None] * direction
        residual = residual - alpha[:, None] * image
        power_next = jnp.sum(residual * residual, axis=1)
        direction = residual + (power_next / power)[:, None] * direction
        power = power_next
    return delta


def local(local_x, dual_var, consensus_old, blocks_data, row_index, labels):
    iterate = local_x[0]
    dual_local = dual_var[0]
    block_rows = blocks_data[0]
    index_rows = row_index[0]
    targets = labels[0].astype(jnp.float32)
    samples = targets.shape[0]
    target = consensus_old - dual_local
    flat_index = index_rows.reshape(-1)
    identity = jnp.eye(iterate.shape[1], dtype=jnp.float32)
    for newton_step in range(NEWTON_STEPS):
        rounded = iterate.astype(jnp.bfloat16)
        partial_value = jnp.einsum(
            "brk,bk->br", block_rows, rounded, preferred_element_type=jnp.float32
        )
        local_margins = jax.ops.segment_sum(
            partial_value.reshape(-1), flat_index, num_segments=samples
        )
        margins = total_of(local_margins, FEAT)
        prob = jax.nn.sigmoid(margins)
        misfit = prob - targets
        weights = prob * (1.0 - prob)
        misfit_rows = misfit[index_rows].astype(jnp.bfloat16)
        gradient = jnp.einsum(
            "brk,br->bk", block_rows, misfit_rows, preferred_element_type=jnp.float32
        )
        gradient = gradient + penalty * (iterate - target)
        weighted = (block_rows * weights[index_rows][:, :, None]).astype(jnp.bfloat16)
        hessian = (
            jnp.einsum("brk,brl->bkl", block_rows, weighted, preferred_element_type=jnp.float32)
            + penalty * identity
        )
        delta = conjugate_solve(hessian, gradient)
        iterate = iterate - damping * delta
    shards = lax.axis_size(("row", "col"))
    combined = iterate + dual_local
    totals = of_everyone(combined, ("row", "col"))
    consensus = shrink(totals / jnp.float32(shards))
    dual_next = dual_local + iterate - consensus
    primal_local = jnp.sum((iterate - consensus) ** 2)
    change_local = jnp.sum((consensus - consensus_old) ** 2)
    primal_total, change_total = (
        by_axis(primal_local, FEAT_ROW_COL),
        by_axis(change_local / jnp.float32(shards), FEAT_ROW_COL),
    )
    norms = jnp.stack(
        [jnp.sqrt(primal_total), penalty * jnp.sqrt(jnp.float32(shards) * change_total)]
    )
    return (iterate[None], dual_next[None], consensus, norms)


def solution(mesh):
    torus = Mesh(
        mesh.devices.reshape(8, 4, 2, mesh.shape["row"], mesh.shape["col"]),
        ("feat_0", "feat_1", "feat_2", "row", "col"),
    )
    placed = (
        P(("row", "col"), FEAT, None),
        P(("row", "col"), FEAT, None),
        P(FEAT, None),
        P(("row", "col"), FEAT, None, None),
        P(("row", "col"), FEAT, None),
        P(("row", "col"), None),
    )
    return jax.shard_map(
        local,
        mesh=torus,
        in_specs=placed,
        out_specs=(
            P(("row", "col"), FEAT, None),
            P(("row", "col"), FEAT, None),
            P(FEAT, None),
            P(),
        ),
        check_vma=False,
    )
```

profile of v0, /device:TPU:1, one launch (start us, length us, event | category | flops | bytes accessed | tf_op | source)
XLA Modules:
  0.0 213.6 jit_solution(8987383086924766513)
XLA Ops:
  0.6 0.0 copy-start.5
  0.6 0.0 copy-start.1
  0.7 0.7 fusion.68
  1.4 1.6 fusion.26
  3.0 0.0 copy-done.5
  3.0 11.8 %scatter_custom_fusion = f32[16384]{0:T(1024)} fusion(s32[2048]{0:T(1024)S(1)} %bitcast.161, f32[2048]{0:T(1024)S(1)} %bitcast.163, f32[]{:T(128)} %constant.9.clone.1), kind=kCustom, calls=%fused_computation.44 | custom fusion | flops 2048 | bytes 65540 | tf_op jit(solution)/shard_map/scatter-add | solution.py:101
  14.8 15.1 %all-to-all-start = ((f32[64,1,256]{2,1,0:T(1,128)}), f32[64,1,256]{2,1,0:T(1,128)S(1)}, u32[]{:S(2)}, u32[]{:S(2)}) async-start(f32[64,1,256]{2,1,0:T(1,128)} %bitcast.4), calls=%async_computation | async-start | bytes 131072 | tf_op jit(solution)/shard_map/all_to_all | solution.py:44
  30.0 11.0 %all-to-all-done = f32[64,1,256]{2,1,0:T(1,128)S(1)} async-done(((f32[64,1,256]{2,1,0:T(1,128)}), f32[64,1,256]{2,1,0:T(1,128)S(1)}, u32[]{:S(2)}, u32[]{:S(2)}) %all-to-all-start) | async-done | bytes 65568 | tf_op jit(solution)/shard_map/all_to_all | solution.py:44
  41.0 0.1 reduce_sum.153
  41.1 0.7 broadcast_in_dim.10
  41.8 4.6 %all-to-all-start.1 = ((f32[64,1,256]{2,1,0:T(1,128)}), f32[64,1,256]{2,1,0:T(1,128)S(1)}, u32[]{:S(2)}, u32[]{:S(2)}) async-start(f32[64,1,256]{2,1,0:T(1,128)} %broadcast_in_dim.10), calls=%async_computation.1 | async-start | bytes 131072 | tf_op jit(solution)/shard_map/all_to_all | solution.py:23
  46.4 0.0 copy-done.1
  46.5 10.9 %all-to-all-done.1 = f32[64,1,256]{2,1,0:T(1,128)S(1)} async-done(((f32[64,1,256]{2,1,0:T(1,128)}), f32[64,1,256]{2,1,0:T(1,128)S(1)}, u32[]{:S(2)}, u32[]{:S(2)}) %all-to-all-start.1) | async-done | bytes 65568 | tf_op jit(solution)/shard_map/all_to_all | solution.py:23
  57.5 11.8 %gather_fusion.1 = f32[2048]{0:T(1024)S(1)} fusion(f32[16384]{0:T(1024)S(1)} %subtract_multiply_fusion.1, s32[2048]{0:T(1024)S(1)} %broadcast_clamp_fusion), kind=kCustom, calls=%fused_computation.1 | custom fusion | bytes 24576 | tf_op jit(solution)/shard_map/gather | solution.py:113
  69.3 0.0 copy-start
  69.3 13.1 %gather_fusion = bf16[2048]{0:T(1024)(128)(2,1)S(1)} fusion(bf16[16384]{0:T(1024)(128)(2,1)S(1)} %sub.52, s32[2048]{0:T(1024)S(1)} %broadcast_clamp_fusion), kind=kCustom, calls=%fused_computation | custom fusion | bytes 16384 | tf_op jit(solution)/shard_map/gather | solution.py:108
  82.4 0.0 copy-done
  82.4 0.2 fusion.24
  82.7 0.9 fusion.9
  83.6 0.0 copy-done.2
  83.6 0.0 copy-done.3
  83.6 0.0 copy-done.4
  83.6 0.7 fusion.65
  84.3 0.1 fusion.52
  84.5 0.2 multiply_reduce_fusion.6
  84.7 0.1 multiply_add_fusion.3
  84.7 0.7 fusion.63
  85.4 0.1 fusion.50
  85.5 0.2 multiply_reduce_fusion.5
  85.7 0.1 multiply_add_fusion.2
  85.8 0.7 fusion.61
  86.5 0.1 fusion.49
  86.6 0.1 convert_bitcast_fusion
  86.7 0.4 fusion.20
  87.1 11.3 %scatter_custom_fusion.1 = f32[16384]{0:T(1024)S(1)} fusion(s32[2048]{0:T(1024)S(1)} %bitcast.162, f32[2048]{0:T(1024)S(1)} %bitcast.164, f32[]{:T(128)} %constant.9.clone.1), kind=kCustom, calls=%fused_computation.42 | custom fusion | flops 2048 | bytes 65540 | tf_op jit(solution)/shard_map/scatter-add | solution.py:101
  98.4 14.8 %all_to_all.35 = f32[64,1,256]{2,1,0:T(1,128)S(1)} all-to-all(f32[64,1,256]{2,1,0:T(1,128)S(1)} %bitcast.149), channel_id=1, replica_groups=mesh['feat_0'=8,'feat_1'=4,'feat_2'=2,'row'=2,'col'=2] {'feat_0','feat_1..., dimensions={0} | all-to-all | bytes 131072 | tf_op jit(solution)/shard_map/all_to_all | solution.py:44
  113.2 0.1 reduce_sum.160
  113.3 14.8 %all_to_all.36 = f32[64,1,256]{2,1,0:T(1,128)S(1)} all-to-all(f32[64,1,256]{2,1,0:T(1,128)S(1)} %broadcast_in_dim.11), channel_id=1, replica_groups=mesh['feat_0'=8,'feat_1'=4,'feat_2'=2,'row'=2,'col'=2] {'feat_0','feat_1..., dimensions={0} | all-to-all | bytes 131072 | tf_op jit(solution)/shard_map/all_to_all | solution.py:23
  128.2 13.1 %gather_fusion.2 = bf16[2048]{0:T(1024)(128)(2,1)S(1)} fusion(bf16[16384]{0:T(1024)(128)(2,1)S(1)} %sub.59, s32[2048]{0:T(1024)S(1)} %broadcast_clamp_fusion), kind=kCustom, calls=%fused_computation.2 | custom fusion | bytes 16384 | tf_op jit(solution)/shard_map/gather | solution.py:108
  141.3 11.8 %gather_fusion.3 = f32[2048]{0:T(1024)S(1)} fusion(f32[16384]{0:T(1024)S(1)} %subtract_multiply_fusion, s32[2048]{0:T(1024)S(1)} %broadcast_clamp_fusion), kind=kCustom, calls=%fused_computation.3 | custom fusion | bytes 24576 | tf_op jit(solution)/shard_map/gather | solution.py:113
  153.1 0.2 fusion.18
  153.3 0.9 fusion.15
  154.3 0.7 fusion.58
  155.0 0.1 fusion.47
  155.1 0.2 multiply_reduce_fusion.3
  155.3 0.1 multiply_add_fusion.1
  155.4 0.7 fusion.56
  156.1 0.1 fusion.45
  156.2 0.2 multiply_reduce_fusion.2
  156.4 0.1 multiply_add_fusion
  156.5 0.7 fusion.54
  157.1 0.1 fusion.44
  157.3 0.1 bitcast_add_fusion.1
  157.3 11.1 %all_to_all.37 = f32[4,4,256]{2,1,0:T(4,128)S(1)} all-to-all(f32[4,4,256]{2,1,0:T(4,128)S(1)} %broadcast_in_dim.13), channel_id=1, replica_groups=mesh['feat_0'=8,'feat_1'=4,'feat_2'=2,'row'=2,'col'=2] {'row','col'}, dimensions={0} | all-to-all | bytes 32768 | tf_op jit(solution)/shard_map/all_to_all | solution.py:23
  168.5 0.7 multiply_reduce_fusion.1
  169.2 0.6 subtract_bitcast_fusion
  170.5 11.9 %all-reduce = (f32[]{:T(128)}, f32[]{:T(128)}) all-reduce(f32[]{:T(128)S(6)} %div.107, f32[]{:T(128)} %get-tuple-element.4), channel_id=1, replica_groups=mesh['feat_0'=8,'feat_1'=4,'feat_2'=2,'row'=2,'col'=2] {'feat_0'}, use_global_device_ids=true, to_apply=%region_24.25 | all-reduce | flops 2 | bytes 16 | tf_op jit(solution)/shard_map/psum | solution.py:62
  182.4 7.4 %all-reduce.1 = (f32[]{:T(128)}, f32[]{:T(128)}) all-reduce(f32[]{:T(128)} %get-tuple-element.10, f32[]{:T(128)} %get-tuple-element.11), channel_id=1, replica_groups=mesh['feat_0'=8,'feat_1'=4,'feat_2'=2,'row'=2,'col'=2] {'feat_1'}, use_global_device_ids=true, to_apply=%region_25.26 | all-reduce | flops 2 | bytes 16 | tf_op jit(solution)/shard_map/psum | solution.py:62
  189.8 5.9 %all-reduce.4 = (f32[]{:T(128)}, f32[]{:T(128)}) all-reduce(f32[]{:T(128)} %get-tuple-element.12, f32[]{:T(128)} %get-tuple-element.13), channel_id=1, replica_groups=mesh['feat_0'=8,'feat_1'=4,'feat_2'=2,'row'=2,'col'=2] {'feat_2'}, use_global_device_ids=true, to_apply=%region_26.27 | all-reduce | flops 2 | bytes 16 | tf_op jit(solution)/shard_map/psum | solution.py:62
  195.7 4.5 %all-reduce.3 = (f32[]{:T(128)}, f32[]{:T(128)}) all-reduce(f32[]{:T(128)} %get-tuple-element.18, f32[]{:T(128)} %get-tuple-element.19), channel_id=1, replica_groups=mesh['feat_0'=8,'feat_1'=4,'feat_2'=2,'row'=2,'col'=2] {'row'}, use_global_device_ids=true, to_apply=%region_27.28 | all-reduce | flops 2 | bytes 16 | tf_op jit(solution)/shard_map/psum | solution.py:62
  200.1 11.6 %all-reduce.2 = (f32[]{:T(128)}, f32[]{:T(128)}) all-reduce(f32[]{:T(128)} %get-tuple-element.16, f32[]{:T(128)} %get-tuple-element.17), channel_id=1, replica_groups=mesh['feat_0'=8,'feat_1'=4,'feat_2'=2,'row'=2,'col'=2] {'col'}, use_global_device_ids=true, to_apply=%region_28.29 | all-reduce | flops 2 | bytes 16 | tf_op jit(solution)/shard_map/psum | solution.py:62
  213.0 0.6 pad_maximum_fusion
  213.6 0.0 copy-done.7
  213.6 0.0 copy-done.6
  (42 shorter events, 0.5 us)
Async XLA Ops:
  0.6 2.4 %copy-start.5 = (s32[1,4,512]{2,1,0:T(4,128)S(1)}, s32[1,4,512]{2,1,0:T(4,128)}, u32[]{:S(2)}) copy-start(s32[1,4,512]{2,1,0:T(4,128)} %param.10) | copy-start | bytes 24580
  0.6 45.8 %copy-start.1 = (s32[1,16384]{1,0:T(1,128)S(1)}, s32[1,16384]{1,0:T(1,128)}, u32[]{:S(2)}) copy-start(s32[1,16384]{1,0:T(1,128)} %param.11) | copy-start | bytes 196612
  14.8 26.2 %all-to-all-start = ((f32[64,1,256]{2,1,0:T(1,128)}), f32[64,1,256]{2,1,0:T(1,128)S(1)}, u32[]{:S(2)}, u32[]{:S(2)}) async-start(f32[64,1,256]{2,1,0:T(1,128)} %bitcast.4), calls=%async_computation | async-start | bytes 131072 | tf_op jit(solution)/shard_map/all_to_all | solution.py:44
  41.8 15.6 %all-to-all-start.1 = ((f32[64,1,256]{2,1,0:T(1,128)}), f32[64,1,256]{2,1,0:T(1,128)S(1)}, u32[]{:S(2)}, u32[]{:S(2)}) async-start(f32[64,1,256]{2,1,0:T(1,128)} %broadcast_in_dim.10), calls=%async_computation.1 | async-start | bytes 131072 | tf_op jit(solution)/shard_map/all_to_all | solution.py:23
  69.3 13.1 %copy-start = (bf16[1,4,512,256]{3,2,1,0:T(8,128)(2,1)S(1)}, bf16[1,4,512,256]{3,2,1,0:T(8,128)(2,1)}, u32[]{:S(2)}) copy-start(bf16[1,4,512,256]{3,2,1,0:T(8,128)(2,1)} %param.9) | copy-start | bytes 3145732
  82.7 0.9 copy-start.2
  82.7 1.0 copy-start.3
  82.7 1.0 copy-start.4
  157.3 56.2 %copy-start.7 = (f32[4,256]{1,0:T(4,128)}, f32[4,256]{1,0:T(4,128)S(1)}, u32[]{:S(2)}) copy-start(f32[4,256]{1,0:T(4,128)S(1)} %get-tuple-element.22) | copy-start | bytes 12292
  169.2 44.4 %copy-start.6 = (f32[4,256]{1,0:T(4,128)}, f32[4,256]{1,0:T(4,128)S(1)}, u32[]{:S(2)}) copy-start(f32[4,256]{1,0:T(4,128)S(1)} %get-tuple-element.20) | copy-start | bytes 12292
where the time goes:
time: 214 us
  blocking collectives  81.9 us (38%)
  local copies, waits for them, and re-layouts  50.6 us (24%)
  other arithmetic  28.1 us (13%)
  waiting for transfers between devices  21.9 us (10%)
  starting transfers between devices  19.7 us (9%)
  matrix products  8.28 us (4%)
  between operations  3 us (1%)
    psum x5, blocking collectives, by_axis(): x = lax.psum(x, axis)  41.2 us
    gather x2, local copies, waits for them, and re-layouts, local(): misfit_rows = misfit[index_rows].astype(jnp.bfloat16)  26.2 us
    all_to_all x2, blocking collectives, copy_for_each(): return lax.all_to_all(copies, axis, split_axis=0, concat_axis=0, tiled=True)  25.9 us
    gather x4, local copies, waits for them, and re-layouts, local(): weights[index_rows][:, :, None]  23.6 us
    scatter-add x2, other arithmetic, local(): jax.ops.segment_sum(partial_value.reshape(-1), flat_index, num_segments=s...  23.1 us
    all_to_all x1, starting transfers between devices, summed_on_arrival(): parts = lax.all_to_all(cut_along(x, dim, size), axis, 0, 0, tiled=True)  15.1 us
    all_to_all x1, blocking collectives, summed_on_arrival(): parts = lax.all_to_all(cut_along(x, dim, size), axis, 0, 0, tiled=True)  14.8 us
    all_to_all x1, waiting for transfers between devices, summed_on_arrival(): parts = lax.all_to_all(cut_along(x, dim, size), axis, 0, 0, tiled=True)  11 us
  transfers between devices with their start and end apart: 2, of which 2 were waited for; matrix products, arithmetic and copies ran while one was open for 0% of the time, Pallas kernels for 0%

commit v1 on v0

--- a/solution.py
+++ b/solution.py
@@ -59,7 +59,7 @@
 
 def by_axis(x, axes):
     for axis in axes:
-        x = lax.psum(x, axis)
+        x = jax.lax.all_gather(x, axis_name=axis).sum(axis=0)
     return x
 
 

time: 214 us -> 235 us (1.098)
  local copies, waits for them, and re-layouts: 50.6 us -> 68.3 us
  blocking collectives: 81.9 us -> 67.4 us
  starting transfers between devices: 19.7 us -> 28.6 us
  other arithmetic: 28.1 us -> 34.4 us
  waiting for transfers between devices: 21.9 us -> 24.5 us
    psum x5 -> x0, blocking collectives: 41.2 us -> none  [by_axis(): x = lax.psum(x, axis)]
    unnamed x0 -> x5, blocking collectives: none -> 37.8 us
    unnamed x22 -> x57, local copies, waits for them, and re-layouts: 0.13 us -> 17.2 us
    all_to_all x2 -> x1, blocking collectives: 25.9 us -> 14.8 us  [copy_for_each(): return lax.all_to_all(copies, axis, split_axis=0, concat_axis=0, tiled=True)]
    all_to_all x1 -> x2, starting transfers between devices: 4.61 us -> 13.5 us  [copy_for_each(): return lax.all_to_all(copies, axis, split_axis=0, concat_axis=0, tiled=True)]
    reduce_sum x0 -> x10, other arithmetic: none -> 6.33 us  [by_axis(): x = jax.lax.all_gather(x, axis_name=axis).sum(axis=0)]
    all_to_all x1 -> x2, waiting for transfers between devices: 10.9 us -> 13.4 us  [copy_for_each(): return lax.all_to_all(copies, axis, split_axis=0, concat_axis=0, tiled=True)]
  transfers between devices with their start and end apart: 2 -> 3, of which waited for: 2 -> 3; matrix products, arithmetic and copies ran while one was open for 0% -> 0% of each run, Pallas kernels for 0% -> 0%
where the time goes in v1:
time: 235 us; the launch traced here: 234 us
  local copies, waits for them, and re-layouts  68.3 us (29%)
  blocking collectives  67.4 us (29%)
  other arithmetic  34.4 us (15%)
  starting transfers between devices  28.6 us (12%)
  waiting for transfers between devices  24.5 us (10%)
  matrix products  8.26 us (4%)
  between operations  3.1 us (1%)
    unnamed x5, blocking collectives  37.8 us
    gather x2, local copies, waits for them, and re-layouts, local(): misfit_rows = misfit[index_rows].astype(jnp.bfloat16)  26.2 us
    gather x4, local copies, waits for them, and re-layouts, local(): weights[index_rows][:, :, None]  23.6 us
    scatter-add x2, other arithmetic, local(): jax.ops.segment_sum(partial_value.reshape(-1), flat_index, num_segments=s...  23.1 us
    unnamed x57, local copies, waits for them, and re-layouts  17.2 us
    all_to_all x1, starting transfers between devices, summed_on_arrival(): parts = lax.all_to_all(cut_along(x, dim, size), axis, 0, 0, tiled=True)  15.1 us
    all_to_all x1, blocking collectives, copy_for_each(): return lax.all_to_all(copies, axis, split_axis=0, concat_axis=0, tiled=True)  14.8 us
    all_to_all x1, blocking collectives, summed_on_arrival(): parts = lax.all_to_all(cut_along(x, dim, size), axis, 0, 0, tiled=True)  14.8 us
  transfers between devices with their start and end apart: 3, of which 3 were waited for; matrix products, arithmetic and copies ran while one was open for 0% of the time, Pallas kernels for 0%

profile of v1, /device:TPU:1, one launch (start us, length us, event | category | flops | bytes accessed | tf_op | source)
XLA Modules:
  0.0 234.5 jit_solution(4961738599127957706)
XLA Ops:
  0.7 0.8 copy.54
  1.4 0.7 fusion.68
  2.1 1.6 fusion.26
  3.7 11.8 %scatter_custom_fusion = f32[16384]{0:T(1024)} fusion(s32[2048]{0:T(1024)S(1)} %bitcast.176, f32[2048]{0:T(1024)S(1)} %bitcast.179, f32[]{:T(128)} %constant.9.clone.1), kind=kCustom, calls=%fused_computation.44 | custom fusion | flops 2048 | bytes 65540 | tf_op jit(solution)/shard_map/scatter-add | solution.py:101
  15.5 15.1 %all-to-all-start = ((f32[64,1,256]{2,1,0:T(1,128)}), f32[64,1,256]{2,1,0:T(1,128)S(1)}, u32[]{:S(2)}, u32[]{:S(2)}) async-start(f32[64,1,256]{2,1,0:T(1,128)} %bitcast.4), calls=%async_computation | async-start | bytes 131072 | tf_op jit(solution)/shard_map/all_to_all | solution.py:44
  30.7 11.0 %all-to-all-done = f32[64,1,256]{2,1,0:T(1,128)S(1)} async-done(((f32[64,1,256]{2,1,0:T(1,128)}), f32[64,1,256]{2,1,0:T(1,128)S(1)}, u32[]{:S(2)}, u32[]{:S(2)}) %all-to-all-start) | async-done | bytes 65568 | tf_op jit(solution)/shard_map/all_to_all | solution.py:44
  41.8 0.7 broadcast_in_dim.10
  42.5 4.6 %all-to-all-start.1 = ((f32[64,1,256]{2,1,0:T(1,128)}), f32[64,1,256]{2,1,0:T(1,128)S(1)}, u32[]{:S(2)}, u32[]{:S(2)}) async-start(f32[64,1,256]{2,1,0:T(1,128)} %broadcast_in_dim.10), calls=%async_computation.1 | async-start | bytes 131072 | tf_op jit(solution)/shard_map/all_to_all | solution.py:23
  47.2 10.9 %all-to-all-done.1 = f32[64,1,256]{2,1,0:T(1,128)S(1)} async-done(((f32[64,1,256]{2,1,0:T(1,128)}), f32[64,1,256]{2,1,0:T(1,128)S(1)}, u32[]{:S(2)}, u32[]{:S(2)}) %all-to-all-start.1) | async-done | bytes 65568 | tf_op jit(solution)/shard_map/all_to_all | solution.py:23
  58.2 13.1 %gather_fusion = bf16[2048]{0:T(1024)(128)(2,1)S(1)} fusion(bf16[16384]{0:T(1024)(128)(2,1)S(1)} %sub.52, s32[2048]{0:T(1024)S(1)} %broadcast_clamp_fusion), kind=kCustom, calls=%fused_computation | custom fusion | bytes 16384 | tf_op jit(solution)/shard_map/gather | solution.py:108
  71.3 0.2 fusion.24
  71.6 11.8 %gather_fusion.1 = f32[2048]{0:T(1024)S(1)} fusion(f32[16384]{0:T(1024)S(1)} %subtract_multiply_fusion.1, s32[2048]{0:T(1024)S(1)} %broadcast_clamp_fusion), kind=kCustom, calls=%fused_computation.1 | custom fusion | bytes 24576 | tf_op jit(solution)/shard_map/gather | solution.py:113
  83.4 0.9 fusion.9
  84.4 0.7 fusion.65
  85.5 0.7 fusion.63
  86.5 0.7 fusion.61
  87.4 0.4 fusion.20
  87.8 11.3 %scatter_custom_fusion.1 = f32[16384]{0:T(1024)S(1)} fusion(s32[2048]{0:T(1024)S(1)} %bitcast.177, f32[2048]{0:T(1024)S(1)} %bitcast.178, f32[]{:T(128)} %constant.9.clone.1), kind=kCustom, calls=%fused_computation.42 | custom fusion | flops 2048 | bytes 65540 | tf_op jit(solution)/shard_map/scatter-add | solution.py:101
  99.1 14.8 %all_to_all.36 = f32[64,1,256]{2,1,0:T(1,128)S(1)} all-to-all(f32[64,1,256]{2,1,0:T(1,128)S(1)} %bitcast.164), channel_id=1, replica_groups=mesh['feat_0'=8,'feat_1'=4,'feat_2'=2,'row'=2,'col'=2] {'feat_0','feat_1..., dimensions={0} | all-to-all | bytes 131072 | tf_op jit(solution)/shard_map/all_to_all | solution.py:44
  114.0 14.8 %all_to_all.35 = f32[64,1,256]{2,1,0:T(1,128)S(1)} all-to-all(f32[64,1,256]{2,1,0:T(1,128)S(1)} %broadcast_in_dim.11), channel_id=1, replica_groups=mesh['feat_0'=8,'feat_1'=4,'feat_2'=2,'row'=2,'col'=2] {'feat_0','feat_1..., dimensions={0} | all-to-all | bytes 131072 | tf_op jit(solution)/shard_map/all_to_all | solution.py:23
  128.9 13.1 %gather_fusion.2 = bf16[2048]{0:T(1024)(128)(2,1)S(1)} fusion(bf16[16384]{0:T(1024)(128)(2,1)S(1)} %sub.59, s32[2048]{0:T(1024)S(1)} %broadcast_clamp_fusion), kind=kCustom, calls=%fused_computation.2 | custom fusion | bytes 16384 | tf_op jit(solution)/shard_map/gather | solution.py:108
  142.0 0.2 fusion.18
  142.3 11.8 %gather_fusion.3 = f32[2048]{0:T(1024)S(1)} fusion(f32[16384]{0:T(1024)S(1)} %subtract_multiply_fusion, s32[2048]{0:T(1024)S(1)} %broadcast_clamp_fusion), kind=kCustom, calls=%fused_computation.3 | custom fusion | bytes 24576 | tf_op jit(solution)/shard_map/gather | solution.py:113
  154.1 0.9 fusion.15
  155.0 0.7 fusion.58
  156.1 0.7 fusion.56
  156.9 0.2 multiply_reduce_fusion.2
  157.2 0.7 fusion.54
  158.1 0.6 broadcast_in_dim.13
  158.7 8.9 %all-to-all-start.4 = ((f32[4,4,256]{2,1,0:T(4,128)}), f32[4,4,256]{2,1,0:T(4,128)S(1)}, u32[]{:S(2)}, u32[]{:S(2)}) async-start(f32[4,4,256]{2,1,0:T(4,128)} %broadcast_in_dim.13), calls=%async_computation.4 | async-start | bytes 32768 | tf_op jit(solution)/shard_map/all_to_all | solution.py:23
  167.5 0.6 dynamic-slice
  168.1 2.6 %all-to-all-done.4 = f32[4,4,256]{2,1,0:T(4,128)S(1)} async-done(((f32[4,4,256]{2,1,0:T(4,128)}), f32[4,4,256]{2,1,0:T(4,128)S(1)}, u32[]{:S(2)}, u32[]{:S(2)}) %all-to-all-start.4) | async-done | bytes 16416 | tf_op jit(solution)/shard_map/all_to_all | solution.py:23
  170.7 0.6 multiply_reduce_fusion.1
  172.0 0.7 dynamic-update-slice.5
  172.6 1.3 dynamic-update-slice
  174.0 0.6 dynamic-slice.1
  174.5 11.2 %all-reduce.10 = (f32[8]{0:T(128)S(1)}, f32[8]{0:T(128)S(1)}) all-reduce(f32[8]{0:T(128)S(1)} %dynamic-update-slice.5, f32[8]{0:T(128)S(1)} %dynamic-update-slice), channel_id=1, replica_groups=mesh['feat_0'=8,'feat_1'=4,'feat_2'=2,'row'=2,'col'=2] {'feat_0'}, use_global_device_ids=true, to_apply=%add.5 | all-reduce | flops 16 | bytes 128
  185.8 0.6 reduce_sum.265
  186.4 0.7 reduce_sum.259
  187.0 1.4 dynamic-update-slice.6
  188.5 1.4 dynamic-update-slice.1
  189.9 0.6 dynamic-slice.2
  190.5 6.7 %all-reduce.11 = (f32[4]{0:T(128)S(1)}, f32[4]{0:T(128)S(1)}) all-reduce(f32[4]{0:T(128)S(1)} %dynamic-update-slice.6, f32[4]{0:T(128)S(1)} %dynamic-update-slice.1), channel_id=1, replica_groups=mesh['feat_0'=8,'feat_1'=4,'feat_2'=2,'row'=2,'col'=2] {'feat_1'}, use_global_device_ids=true, to_apply=%add.6 | all-reduce | flops 8 | bytes 64
  197.2 0.6 reduce_sum.266
  197.8 0.7 reduce_sum.260
  198.5 1.4 dynamic-update-slice.7
  199.9 1.4 dynamic-update-slice.2
  201.3 0.6 dynamic-slice.3
  201.9 5.3 %all-reduce.14 = (f32[2]{0:T(128)S(1)}, f32[2]{0:T(128)S(1)}) all-reduce(f32[2]{0:T(128)S(1)} %dynamic-update-slice.7, f32[2]{0:T(128)S(1)} %dynamic-update-slice.2), channel_id=1, replica_groups=mesh['feat_0'=8,'feat_1'=4,'feat_2'=2,'row'=2,'col'=2] {'feat_2'}, use_global_device_ids=true, to_apply=%add.7 | all-reduce | flops 4 | bytes 32
  207.2 0.6 reduce_sum.267
  207.8 0.7 reduce_sum.261
  208.4 1.4 dynamic-update-slice.8
  209.8 1.4 dynamic-update-slice.3
  211.3 0.6 dynamic-slice.4
  211.9 3.8 %all-reduce.13 = (f32[2]{0:T(128)S(1)}, f32[2]{0:T(128)S(1)}) all-reduce(f32[2]{0:T(128)S(1)} %dynamic-update-slice.8, f32[2]{0:T(128)S(1)} %dynamic-update-slice.3), channel_id=1, replica_groups=mesh['feat_0'=8,'feat_1'=4,'feat_2'=2,'row'=2,'col'=2] {'row'}, use_global_device_ids=true, to_apply=%add.8 | all-reduce | flops 4 | bytes 32
  215.6 0.6 reduce_sum.268
  216.2 0.7 reduce_sum.262
  216.9 1.4 dynamic-update-slice.9
  218.3 1.4 dynamic-update-slice.4
  219.8 0.6 subtract_bitcast_fusion
  220.4 10.9 %all-reduce.12 = (f32[2]{0:T(128)S(1)}, f32[2]{0:T(128)S(1)}) all-reduce(f32[2]{0:T(128)S(1)} %dynamic-update-slice.9, f32[2]{0:T(128)S(1)} %dynamic-update-slice.4), channel_id=1, replica_groups=mesh['feat_0'=8,'feat_1'=4,'feat_2'=2,'row'=2,'col'=2] {'col'}, use_global_device_ids=true, to_apply=%add.9 | all-reduce | flops 4 | bytes 32
  231.3 0.6 reduce_sum.269
  232.6 0.6 reduce_sum.263
  233.9 0.6 pad_maximum_fusion
  (88 shorter events, 2.5 us)
Async XLA Ops:
  0.6 30.0 %copy-start.5 = (s32[1,4,512]{2,1,0:T(4,128)S(1)}, s32[1,4,512]{2,1,0:T(4,128)}, u32[]{:S(2)}) copy-start(s32[1,4,512]{2,1,0:T(4,128)} %param.10) | copy-start | bytes 24580
  0.6 46.5 %copy-start.1 = (s32[1,16384]{1,0:T(1,128)S(1)}, s32[1,16384]{1,0:T(1,128)}, u32[]{:S(2)}) copy-start(s32[1,16384]{1,0:T(1,128)} %param.11) | copy-start | bytes 196612
  15.5 26.2 %all-to-all-start = ((f32[64,1,256]{2,1,0:T(1,128)}), f32[64,1,256]{2,1,0:T(1,128)S(1)}, u32[]{:S(2)}, u32[]{:S(2)}) async-start(f32[64,1,256]{2,1,0:T(1,128)} %bitcast.4), calls=%async_computation | async-start | bytes 131072 | tf_op jit(solution)/shard_map/all_to_all | solution.py:44
  42.5 15.6 %all-to-all-start.1 = ((f32[64,1,256]{2,1,0:T(1,128)}), f32[64,1,256]{2,1,0:T(1,128)S(1)}, u32[]{:S(2)}, u32[]{:S(2)}) async-start(f32[64,1,256]{2,1,0:T(1,128)} %broadcast_in_dim.10), calls=%async_computation.1 | async-start | bytes 131072 | tf_op jit(solution)/shard_map/all_to_all | solution.py:23
  58.2 13.1 %copy-start = (bf16[1,4,512,256]{3,2,1,0:T(8,128)(2,1)S(1)}, bf16[1,4,512,256]{3,2,1,0:T(8,128)(2,1)}, u32[]{:S(2)}) copy-start(bf16[1,4,512,256]{3,2,1,0:T(8,128)(2,1)} %param.9) | copy-start | bytes 3145732
  83.4 1.0 copy-start.2
  83.4 1.0 copy-start.3
  83.4 1.0 copy-start.4
  156.1 11.4 %copy-start.12 = (u32[256]{0:T(256)S(1)}, u32[256]{0:T(256)}, u32[]{:S(2)}) copy-start(u32[256]{0:T(256)} %constant.30) | copy-start | bytes 3076
  156.1 17.8 %copy-start.11 = (u32[256]{0:T(256)S(1)}, u32[256]{0:T(256)}, u32[]{:S(2)}) copy-start(u32[256]{0:T(256)} %constant.35) | copy-start | bytes 3076
  156.1 33.8 %copy-start.10 = (u32[256]{0:T(256)S(1)}, u32[256]{0:T(256)}, u32[]{:S(2)}) copy-start(u32[256]{0:T(256)} %constant.40) | copy-start | bytes 3076
  156.1 45.2 %copy-start.9 = (u32[256]{0:T(256)S(1)}, u32[256]{0:T(256)}, u32[]{:S(2)}) copy-start(u32[256]{0:T(256)} %constant.45) | copy-start | bytes 3076
  156.1 55.2 %copy-start.8 = (u32[256]{0:T(256)S(1)}, u32[256]{0:T(256)}, u32[]{:S(2)}) copy-start(u32[256]{0:T(256)} %constant.50) | copy-start | bytes 3076
  158.1 76.4 %copy-start.7 = (f32[4,256]{1,0:T(4,128)}, f32[4,256]{1,0:T(4,128)S(1)}, u32[]{:S(2)}) copy-start(f32[4,256]{1,0:T(4,128)S(1)} %get-tuple-element.22) | copy-start | bytes 12292
  158.7 12.0 %all-to-all-start.4 = ((f32[4,4,256]{2,1,0:T(4,128)}), f32[4,4,256]{2,1,0:T(4,128)S(1)}, u32[]{:S(2)}, u32[]{:S(2)}) async-start(f32[4,4,256]{2,1,0:T(4,128)} %broadcast_in_dim.13), calls=%async_computation.4 | async-start | bytes 32768 | tf_op jit(solution)/shard_map/all_to_all | solution.py:23
  171.3 63.2 %copy-start.6 = (f32[4,256]{1,0:T(4,128)}, f32[4,256]{1,0:T(4,128)S(1)}, u32[]{:S(2)}) copy-start(f32[4,256]{1,0:T(4,128)S(1)} %get-tuple-element.20) | copy-start | bytes 12292
